TPU v7x, 32 devices: a 4x4x1 block of a 4x4x8 slice. The times are simulated.
32 devices in a mesh: dp: 1 (over z), ey: 4 (over y), ex: 4 (over x), core: 2 (over core).
Axes of the slice: x: 4, y: 4, z: 1, core: 2. Of those that a mesh axis runs over, the one named last changes fastest.
The devices are a block of a 4x4x8 slice.
Arguments:
- tokens: bfloat16 [24576, 2048], P(('dp', 'ey', 'ex', 'core'))
- expert_ids: int32 [24576, 8], P(('dp', 'ey', 'ex', 'core'))
- gate_prob: float32 [24576, 8], P(('dp', 'ey', 'ex', 'core'))
- w_gate: bfloat16 [64, 2048, 1024], P(('ey', 'ex', 'core'))
- w_up: bfloat16 [64, 2048, 1024], P(('ey', 'ex', 'core'))
- w_down: bfloat16 [64, 1024, 2048], P(('ey', 'ex', 'core'))
Outputs:
- output: bfloat16 [24576, 2048], P(('dp', 'ey', 'ex', 'core'))
All inputs are finite; a program needn't handle non-finite values.
Results may differ from a plain program's by a relative error of at most 0.0116772.
Values are sent between devices in bfloat16 or wider.
A program may use at most 768 MiB of HBM per device.

v0:
```python
import functools

import jax
import jax.numpy as jnp
from jax import lax
from jax.experimental import pallas as pl
from jax.experimental.pallas import tpu as pltpu
from jax.sharding import PartitionSpec as P

TOKEN_SPEC = P(('dp', 'ey', 'ex', 'core'), None)
EXPERT_SPEC = P(('ey', 'ex', 'core'), None, None)
F32 = jnp.float32
BF16 = jnp.bfloat16
VMEM_LIMIT = 62 * 1024 * 1024
MESH = pl.DeviceIdType.MESH
AXES = (('ex', 'ey'), ('ey', 'ex'))


def target_chips(grid_y, grid_x):
    half_y, half_x = grid_y // 2, grid_x // 2
    chip_list = []
    for chip_y in range(grid_y):
        for chip_x in range(grid_x):
            if chip_y == 0 and chip_x < half_x:
                chip_list.append(half_y * grid_x + chip_x + half_x)
            elif chip_y == half_y and chip_x >= half_x:
                chip_list.append(chip_x - half_x)
            else:
                chip_list.append(chip_y * grid_x + chip_x)
    return chip_list


def is_moved(iy, ix, n):
    half = n // 2
    return ((iy == 0) & (ix < half)) | ((iy == half) & (ix >= half))


def row_to_columns(row):
    return jnp.transpose(jnp.broadcast_to(row, (128, row.shape[1])))


def pick_matrix(row, n_tok):
    cols = row_to_columns(row)
    lane = lax.broadcasted_iota(jnp.int32, cols.shape, 1).astype(F32)
    blocks = [(cols == lane + (128.0 * k)).astype(F32).astype(BF16) for k in range(n_tok // 128)]
    return jnp.concatenate(blocks, axis=1)


def spread_matrix(row, n_tok):
    tok = lax.broadcasted_iota(jnp.int32, (n_tok, row.shape[1]), 0).astype(F32)
    return (tok == row).astype(F32).astype(BF16)


def scaled_rows(rows, gate_row):
    cols = row_to_columns(gate_row)
    reps = rows.shape[1] // 128
    return (rows.astype(F32) * jnp.concatenate([cols] * reps, axis=1)).astype(BF16)


def dot(a, b):
    return jnp.dot(a, b, preferred_element_type=F32)


class Here:
    def __init__(self, n, n_core):
        self.n, self.n_core = n, n_core
        self.iy, self.ix, self.ic = (lax.axis_index(a) for a in ('ey', 'ex', 'core'))
        self.at = {'ey': self.iy, 'ex': self.ix, 'core': self.ic}

    def step(self, axis, by):
        size = self.n_core if axis == 'core' else self.n
        return lax.rem(self.at[axis] + (by % size), size)

    def dev(self, **by):
        return {axis: self.step(axis, k) for axis, k in by.items()}

    def moved(self):
        return is_moved(self.iy, self.ix, self.n)

    def middle(self):
        return is_moved(self.iy, self.step('ex', self.n // 2), self.n)

    def barrier(self):
        sem = pltpu.get_barrier_semaphore()
        peers = [self.dev(**{axis: k, 'core': c}) for axis in ('ey', 'ex') for k in range(1, self.n) for c in range(self.n_core)]
        peers += [self.dev(core=1), self.dev(ey=self.n // 2, ex=self.n // 2)]
        for peer in peers:
            pl.semaphore_signal(sem, inc=1, device_id=peer, device_id_type=MESH)
        pl.semaphore_wait(sem, len(peers))


def remote(src, dst, send_sem, recv_sem, dev):
    return pltpu.make_async_remote_copy(src_ref=src, dst_ref=dst, send_sem=send_sem, recv_sem=recv_sem, device_id=dev, device_id_type=MESH)


def rows_at(start, size):
    return pl.ds(pl.multiple_of(start, size), size)


def load_weights(e, wg_ref, wu_ref, wd_ref, w_ref, sem):
    d_model, d_ff = wg_ref.shape[1:]
    dh = d_model // 2
    copies = [
        pltpu.make_async_copy(wg_ref.at[e], w_ref.at[pl.ds(0, d_model)], sem.at[0]),
        pltpu.make_async_copy(wu_ref.at[e], w_ref.at[pl.ds(d_model, d_model)], sem.at[1]),
        pltpu.make_async_copy(wd_ref.at[e, :, pl.ds(0, dh)], w_ref.at[pl.ds(2 * d_model, d_ff)], sem.at[2]),
        pltpu.make_async_copy(wd_ref.at[e, :, pl.ds(dh, dh)], w_ref.at[pl.ds(2 * d_model + d_ff, d_ff)], sem.at[3]),
    ]
    for c in copies:
        c.start()
    return copies


def gated_mlp(x1, x2, w_ref, d_model, d_ff):
    dh = d_model // 2
    gate = dot(x1, w_ref[0:dh]) + dot(x2, w_ref[dh:d_model])
    up = dot(x1, w_ref[d_model:d_model + dh]) + dot(x2, w_ref[d_model + dh:2 * d_model])
    hidden = (jax.nn.silu(gate) * up).astype(BF16)
    y1 = dot(hidden, w_ref[2 * d_model:2 * d_model + d_ff]).astype(BF16)
    y2 = dot(hidden, w_ref[2 * d_model + d_ff:2 * d_model + 2 * d_ff]).astype(BF16)
    return y1, y2


def place(off, n):
    if isinstance(off, int):
        return off if off < n // 2 else (n - 1 if off == n // 2 else off - 1)
    return jnp.where(off < n // 2, off, jnp.where(off == n // 2, n - 1, off - 1))


def return_copy(here, h, j, src, start, dst, s_sem, r_sem, piece):
    axis = AXES[h][1]
    size = here.n_core
    dev = here.dev(**{axis: here.n - j // size, 'core': j % size})
    return remote(src.at[h, rows_at(start + j * piece, piece)], dst.at[h, rows_at(j * piece, piece)], s_sem.at[h, j], r_sem.at[h, j], dev)


def return_keep(h, src, start, dst, s_sem, piece):
    return pltpu.make_async_copy(src.at[h, pl.ds(start, piece)], dst.at[h, pl.ds(0, piece)], s_sem.at[h, 0])


def base_ffn(here, x_ref, start, dst_ref, w_ref, d_model, d_ff, base_rows, s_sem, r_sem):
    n, n_core = here.n, here.n_core
    piece = n * base_rows

    @pl.loop(0, n * n_core)
    def _(t):
        dc, dy = t // n, lax.rem(t, n)
        j = dy * n_core + dc
        rows1 = rows_at(start + j * piece, piece)
        rows2 = [None] * n
        for dx in range(n):
            rows2[place(dx, n)] = rows_at(start + (dx * n_core + dc) * piece + place(dy, n) * base_rows, base_rows)
        x2 = jnp.concatenate([x_ref[1, r] for r in rows2], axis=0)
        y1, y2 = gated_mlp(x_ref[0, rows1], x2, w_ref, d_model, d_ff)
        x_ref[0, rows1] = y1
        for i in range(n):
            x_ref[1, rows2[i]] = y2[i * base_rows:(i + 1) * base_rows]

        @pl.when(j > 0)
        def _():
            return_copy(here, 0, j, x_ref, start, dst_ref, s_sem, r_sem, piece).start()

        @pl.when(j == 0)
        def _():
            return_keep(0, x_ref, start, dst_ref, s_sem, piece).start()

        @pl.when(dy == n - 1)
        def _():
            for dx in range(n - 1, 0, -1):
                return_copy(here, 1, dx * n_core + dc, x_ref, start, dst_ref, s_sem, r_sem, piece).start()

            @pl.when(dc > 0)
            def _():
                return_copy(here, 1, dc, x_ref, start, dst_ref, s_sem, r_sem, piece).start()

            @pl.when(dc == 0)
            def _():
                return_keep(1, x_ref, start, dst_ref, s_sem, piece).start()


def layer_kernel(n, n_core, exp_dev, base_rows, hot_rows, tok_ref, tx_ref, ht_ref, wg_ref, wu_ref, wd_ref,
                 p0_ref, v_ref, re_ref, q_ref, hs_ref, u_ref, hy_ref,
                 rx_ref, htr_ref, g_ref, hb_ref, m_ref, w_ref,
                 own_sem, w_sem, tab_s, tab_r, g_s, g_r, d_s, d_r, hot_s, hot_r, swap_s, swap_r, x_sem, ret_s, ret_r, sum_s, sum_r, ring_s, ring_r, load_sem):
    here = Here(n, n_core)
    tok_dev, d_model = tok_ref.shape
    d_ff = wg_ref.shape[2]
    dh = d_model // 2
    half = tok_dev // 2
    n_dst = n * n_core
    piece = n * base_rows
    n_row = n_dst * piece
    hot_dev = exp_dev * hot_rows
    land = exp_dev * n_row
    recv0 = land + hot_dev
    far_slot = n // 2
    lo, hi = pl.ds(0, half), pl.ds(half, half)

    def slot(s, part=None):
        return pl.ds(s * tok_dev, tok_dev) if part is None else pl.ds(s * tok_dev + part * half, half)

    own = [pltpu.make_async_copy(tok_ref.at[:, pl.ds(h * dh, dh)], g_ref.at[h, slot(0)], own_sem.at[h]) for h in range(2)]
    for c in own:
        c.start()
    here.barrier()

    tabs = []
    for h in range(2):
        rx_ref[h, 0] = tx_ref[h, 0]
        for k in range(1, n):
            c = remote(tx_ref.at[h, k], rx_ref.at[h, k], tab_s.at[h * n + k], tab_r.at[h * n + k], here.dev(**{AXES[h][0]: k}))
            c.start()
            tabs.append(c)
    moved = here.moved()
    middle = here.middle()
    hot_tab = remote(ht_ref, htr_ref, tab_s.at[0], tab_r.at[0], here.dev(ey=n // 2, ex=n // 2))

    @pl.when(moved)
    def _():
        hot_tab.start()

    @pl.when(jnp.logical_not(moved))
    def _():
        htr_ref[...] = ht_ref[...]

    first = []
    for h in range(2):
        own[h].wait()
        axis = AXES[h][0]
        for i, (s, part, by) in enumerate(((1, 0, 1), (n - 1, 1, -1), (1, 1, 1), (n - 1, 0, -1))):
            c = remote(g_ref.at[h, slot(0, part)], g_ref.at[h, slot(s, part)], g_s.at[h, i], g_r.at[h, i], here.dev(**{axis: by}))
            c.start()
            first.append(c)
    weights = load_weights(0, wg_ref, wu_ref, wd_ref, w_ref, w_sem)
    for c in tabs:
        c.wait_recv()

    def pick(s, start, stop):
        @pl.loop(start, stop)
        def _(m):
            e, h = m // 2, lax.rem(m, 2)
            mat = pick_matrix(rx_ref[h, s, pl.ds(2 * e, 1)], tok_dev)
            picked = dot(mat, g_ref[h, slot(s)]).astype(BF16)
            for j in range(n_dst):
                m_ref[h, rows_at(e * n_row + j * piece + place(s, n) * base_rows, base_rows)] = picked[j * base_rows:(j + 1) * base_rows]

    sends = [[], []]

    def send_rows(e, first_row, size, i, keep):
        for j in range(n_dst - 1, -1 if keep else 0, -1):
            for h in range(2):
                if j:
                    src = m_ref.at[h, pl.ds(e * n_row + j * piece + first_row, size)]
                    dst = m_ref.at[h, pl.ds(recv0 + j * piece + first_row, size)] if e == 0 else re_ref.at[h, pl.ds(j * piece + first_row, size)]
                    c = remote(src, dst, d_s.at[h, e, j, i], d_r.at[h, e, j, i], here.dev(**{AXES[h][1]: j // n_core, 'core': j % n_core}))
                else:
                    dst = m_ref.at[h, pl.ds(recv0, piece)] if e == 0 else re_ref.at[h, pl.ds(0, piece)]
                    c = pltpu.make_async_copy(m_ref.at[h, pl.ds(e * n_row, piece)], dst, d_s.at[h, e, j, i])
                c.start()
                sends[e].append(c)

    pick(0, 0, 2 * exp_dev)
    far = []
    for i, (s, part, by) in enumerate(((1, 0, 1), (n - 1, 1, -1))):
        for h in range(2):
            first[h * 4 + i].wait_recv()
            c = remote(g_ref.at[h, slot(s, part)], g_ref.at[h, slot(far_slot, part)], g_s.at[h, 4 + i], g_r.at[h, 4 + i], here.dev(**{AXES[h][0]: by}))
            c.start()
            far.append(c)
    for i, s in enumerate((1, n - 1)):
        for h in range(2):
            first[h * 4 + 2 + i].wait_recv()
        pick(s, 0, 2 * exp_dev)
    send_rows(0, 0, piece - base_rows, 0, False)
    for c in far:
        c.wait_recv()
    pick(far_slot, 0, 2)
    send_rows(0, piece - base_rows, base_rows, 1, True)

    hot = [remote(g_ref.at[h, slot(far_slot)], hb_ref.at[h], hot_s.at[h], hot_r.at[h], here.dev(**{AXES[h][1]: n // 2})) for h in range(2)]

    @pl.when(middle)
    def _():
        for c in hot:
            c.start()

    pick(far_slot, 2, 2 * exp_dev)
    send_rows(1, 0, piece, 0, True)

    def done_send(c):
        if c.is_remote:
            c.wait_send()

    def done_recv(c):
        if c.is_remote:
            c.wait_recv()
        else:
            c.wait()

    for c in weights:
        c.wait()
    for c in sends[0]:
        done_recv(c)
    base_ffn(here, m_ref, recv0, q_ref.at[0], w_ref, d_model, d_ff, base_rows, ret_s.at[0], ret_r.at[0])

    @pl.when(jnp.logical_not(moved))
    def _():
        for h in range(2):
            hb_ref[h] = g_ref[h, slot(0)]

    @pl.when(moved)
    def _():
        hot_tab.wait_recv()
        for c in hot:
            c.wait_recv()

    for c in sends[0]:
        done_send(c)

    def hot_pick(rel):
        @pl.loop(0, exp_dev)
        def _(e):
            mat = pick_matrix(htr_ref[pl.ds(rel * exp_dev + e, 1)], tok_dev)
            for h in range(2):
                m_ref[h, rows_at(rel * hot_dev + e * hot_rows, hot_rows)] = dot(mat, hb_ref[h]).astype(BF16)

    away, here_rows = pl.ds(hot_dev, hot_dev), pl.ds(land, hot_dev)
    hot_pick(1)
    swap = [remote(m_ref.at[h, away], m_ref.at[h, here_rows], swap_s.at[h], swap_r.at[h], here.dev(core=1)) for h in range(2)]
    back = [remote(m_ref.at[h, here_rows], hy_ref.at[h], swap_s.at[2 + h], swap_r.at[2 + h], here.dev(core=1)) for h in range(2)]
    for c in swap:
        c.start()
    hot_pick(0)
    for c in swap:
        c.wait_recv()
    tiles = hot_rows // piece

    @pl.loop(0, exp_dev)
    def _(e):
        @pl.when(e > 0)
        def _():
            for c in load_weights(e, wg_ref, wu_ref, wd_ref, w_ref, w_sem):
                c.wait()

        @pl.loop(0, n_core * tiles)
        def _(k):
            rows = rows_at((k // tiles) * land + e * hot_rows + lax.rem(k, tiles) * piece, piece)
            y1, y2 = gated_mlp(m_ref[0, rows], m_ref[1, rows], w_ref, d_model, d_ff)
            m_ref[0, rows] = y1
            m_ref[1, rows] = y2

    for c in back:
        c.start()

    for c in sends[1]:
        done_recv(c)
        done_send(c)
    x_in = pltpu.make_async_copy(re_ref, m_ref.at[:, pl.ds(n_row, n_row)], x_sem)
    x_in.start()
    x_in.wait()
    base_ffn(here, m_ref, n_row, q_ref.at[1], w_ref, d_model, d_ff, base_rows, ret_s.at[1], ret_r.at[1])

    for h in range(2):
        return_keep(h, m_ref, recv0, q_ref.at[0], ret_s.at[0], piece).wait()
        for j in range(1, n_dst):
            c = return_copy(here, h, j, m_ref, recv0, q_ref.at[0], ret_s.at[0], ret_r.at[0], piece)
            c.wait_send()
            c.wait_recv()
    q_in = pltpu.make_async_copy(q_ref.at[0], m_ref.at[:, pl.ds(recv0, n_row)], x_sem)
    q_in.start()

    for c in swap:
        c.wait_send()
    hy_in = [pltpu.make_async_copy(hy_ref.at[h], m_ref.at[h, away], own_sem.at[h]) for h in range(2)]
    for h in range(2):
        back[h].wait_recv()
        hy_in[h].start()
    for c in hy_in:
        c.wait()
    kinds = n_core * exp_dev

    @pl.loop(0, 2)
    def _(h):
        acc = None
        for k in range(kinds):
            rows = scaled_rows(m_ref[h, pl.ds(k * hot_rows, hot_rows)], htr_ref[kinds + k:kinds + k + 1])
            term = dot(spread_matrix(htr_ref[k:k + 1], tok_dev), rows)
            acc = term if acc is None else acc + term
        hb_ref[h] = acc.astype(BF16)

    sums = [remote(hb_ref.at[h], hs_ref.at[h], sum_s.at[h], sum_r.at[h], here.dev(**{AXES[h][1]: n // 2})) for h in range(2)]

    @pl.when(moved)
    def _():
        for c in sums:
            c.start()

    for c in first + far:
        c.wait_send()

    @pl.when(middle)
    def _():
        for c in hot:
            c.wait_send()

    def load_piece(h, j):
        rows = pl.ds(j * piece, piece)
        return pltpu.make_async_copy(q_ref.at[1, h, rows], g_ref.at[h, rows], load_sem.at[h, j])

    for h in range(2):
        return_keep(h, m_ref, n_row, q_ref.at[1], ret_s.at[1], piece).wait()
        load_piece(h, 0).start()
    for j in range(n_dst - 1, 0, -1):
        for h in range(2):
            return_copy(here, h, j, m_ref, n_row, q_ref.at[1], ret_s.at[1], ret_r.at[1], piece).wait_recv()
            load_piece(h, j).start()
    q_in.wait()
    for h in range(2):
        for j in range(n_dst):
            load_piece(h, j).wait()

    def p_rows(h, s):
        return rows_at((h * n + s) * tok_dev, tok_dev)

    def p_half(h, s, part):
        return pl.ds((h * n + s) * tok_dev + part * half, half)

    def spread(h, s):
        acc = None
        for e, (ref, start) in enumerate(((m_ref, recv0), (g_ref, 0))):
            rows = jnp.concatenate([ref[h, pl.ds(start + j * piece + place(s, n) * base_rows, base_rows)] for j in range(n_dst)], axis=0)
            term = dot(spread_matrix(rx_ref[h, s, pl.ds(2 * e, 1)], tok_dev), scaled_rows(rows, rx_ref[h, s, pl.ds(2 * e + 1, 1)]))
            acc = term if acc is None else acc + term
        return acc

    ring = []

    def send(h, i, s, part, dst, by, start=True):
        c = remote(w_ref.at[p_half(h, s, part)], dst, ring_s.at[h, i], ring_r.at[h, i], here.dev(**{AXES[h][0]: by}))
        if start:
            c.start()
        ring.append(c)
        return c

    tops = []
    for h in range(2):
        w_ref[p_rows(h, far_slot)] = spread(h, far_slot).astype(BF16)
        tops.append(send(h, 0, far_slot, 0, u_ref.at[h, lo], 1, False))
        tops.append(send(h, 1, far_slot, 1, u_ref.at[h, hi], -1, False))

        @pl.when(jnp.logical_not(middle))
        def _():
            tops[2 * h].start()
            tops[2 * h + 1].start()

    last = []
    for s, part, by in ((n - 1, 1, 1), (1, 0, -1)):
        @pl.loop(0, 2)
        def _(h):
            w_ref[p_rows(h, s)] = spread(h, s).astype(BF16)

        for h in range(2):
            last.append(send(h, 2 + part, s, part, v_ref.at[h, 1 - part, (lo, hi)[part]], by))

    def load(ref, h, rows, start):
        c = pltpu.make_async_copy(ref.at[h, rows], m_ref.at[h, pl.ds(start, half)], own_sem.at[h])
        c.start()
        c.wait()
        return m_ref[h, pl.ds(start, half)].astype(F32)

    def add_to(h, s, part, more):
        rows = p_half(h, s, part)
        w_ref[rows] = (w_ref[rows].astype(F32) + more).astype(BF16)

    @pl.when(middle)
    def _():
        for h in range(2):
            sums[h].wait_recv()
            add_to(h, far_slot, 0, load(hs_ref, h, lo, 0))
            tops[2 * h].start()
            add_to(h, far_slot, 1, load(hs_ref, h, hi, 0))
            tops[2 * h + 1].start()

    own_hot = jnp.where(moved, 0.0, 1.0).astype(F32)

    @pl.loop(0, 2)
    def _(h):
        w_ref[p_rows(h, 0)] = (spread(h, 0) + own_hot * hb_ref[h].astype(F32)).astype(BF16)

    out = [pltpu.make_async_copy(w_ref.at[p_rows(h, 0)], p0_ref.at[h], x_sem) for h in range(2)]
    out[0].start()
    out[0].wait()
    out[1].start()
    for h in range(2):
        tops[2 * h].wait_recv()
        add_to(h, n - 1, 0, load(u_ref, h, lo, 0))
        last.append(send(h, 4, n - 1, 0, v_ref.at[h, 0, lo], 1))
        tops[2 * h + 1].wait_recv()
        add_to(h, 1, 1, load(u_ref, h, hi, 0))
        last.append(send(h, 5, 1, 1, v_ref.at[h, 1, hi], -1))

    out[1].wait()
    for c in tabs + back:
        c.wait_send()
    for h in range(2):
        for j in range(1, n_dst):
            return_copy(here, h, j, m_ref, n_row, q_ref.at[1], ret_s.at[1], ret_r.at[1], piece).wait_send()

    @pl.when(moved)
    def _():
        hot_tab.wait_send()
        for c in sums:
            c.wait_send()

    for c in ring:
        c.wait_send()
    for c in last:
        c.wait_recv()


def layer(n, n_core, base_rows, hot_rows, tokens, tx, ht, w_gate, w_up, w_down):
    tok_dev, d_model = tokens.shape
    exp_dev, _, d_ff = w_gate.shape
    dh = d_model // 2
    n_dst = n * n_core
    n_row = n_dst * n * base_rows
    any_ = pl.BlockSpec(memory_space=pl.ANY)
    vm = pl.BlockSpec(memory_space=pltpu.VMEM)
    dma = pltpu.SemaphoreType.DMA
    hbm = lambda *shape: jax.ShapeDtypeStruct(shape, BF16)
    return pl.pallas_call(
        functools.partial(layer_kernel, n, n_core, exp_dev, base_rows, hot_rows),
        out_shape=(hbm(2, tok_dev, dh), hbm(2, 2, tok_dev, dh), hbm(2, n_row, dh), hbm(exp_dev, 2, n_row, dh), hbm(2, tok_dev, dh), hbm(2, tok_dev, dh), hbm(2, exp_dev * hot_rows, dh)),
        in_specs=[any_, vm, vm, any_, any_, any_],
        out_specs=(any_,) * 7,
        scratch_shapes=[
            pltpu.VMEM(tx.shape, F32),
            pltpu.VMEM(ht.shape, F32),
            pltpu.VMEM((2, n * tok_dev, dh), BF16),
            pltpu.VMEM((2, tok_dev, dh), BF16),
            pltpu.VMEM((2, (exp_dev + 1) * n_row + exp_dev * hot_rows, dh), BF16),
            pltpu.VMEM((max(2 * d_model + 2 * d_ff, 2 * n * tok_dev), dh), BF16),
            dma((2,)), dma((4,)), dma((2 * n,)), dma((2 * n,)), dma((2, 6)), dma((2, 6)),
            dma((2, exp_dev, n_dst, 2)), dma((2, exp_dev, n_dst, 2)), dma((2,)), dma((2,)), dma((4,)), dma((4,)), dma,
            dma((exp_dev, 2, n_dst)), dma((exp_dev, 2, n_dst)), dma((2,)), dma((2,)), dma((2, 6)), dma((2, 6)), dma((2, n_dst)),
        ],
        compiler_params=pltpu.CompilerParams(vmem_limit_bytes=VMEM_LIMIT, collective_id=0, has_side_effects=True),
        name='layer',
    )(tokens, tx, ht, w_gate, w_up, w_down)[:2]


def last_sum_kernel(p_ref, v_ref, out_ref):
    dh = p_ref.shape[-1]
    for h in range(2):
        out_ref[:, h * dh:(h + 1) * dh] = (p_ref[h].astype(F32) + v_ref[h, 0].astype(F32) + v_ref[h, 1].astype(F32)).astype(BF16)


def last_sum(p0, v):
    _, tok_dev, dh = p0.shape
    steps = 6
    rows = tok_dev // steps
    return pl.pallas_call(
        last_sum_kernel,
        grid=(steps,),
        out_shape=jax.ShapeDtypeStruct((tok_dev, 2 * dh), BF16),
        in_specs=[pl.BlockSpec((2, rows, dh), lambda i: (0, i, 0)), pl.BlockSpec((2, 2, rows, dh), lambda i: (0, 0, i, 0))],
        out_specs=pl.BlockSpec((rows, 2 * dh), lambda i: (i, 0)),
        name='last_sum',
    )(p0, v)


def solution(mesh):
    grid_y = mesh.shape['ey']
    grid_x = mesh.shape['ex']
    n_core = mesh.shape['core']
    n = grid_x
    n_dev = grid_y * grid_x * n_core
    chip_list = target_chips(grid_y, grid_x)

    def device_body(tokens, expert_ids, gate_prob, w_gate, w_up, w_down):
        tok_dev, top_k = expert_ids.shape
        exp_dev = w_gate.shape[0]
        exp_chip = exp_dev * n_core
        n_exp = exp_dev * n_dev
        n_copy = tok_dev * top_k
        base_rows = 2 * n_copy // (3 * n_exp)
        hot_rows = grid_y * grid_x * base_rows // 2
        core = lax.axis_index('core')
        iy = lax.axis_index('ey')
        ix = lax.axis_index('ex')
        dst_chip = jnp.where(is_moved(iy, ix, n), lax.rem(iy + n // 2, n) * n + lax.rem(ix + n // 2, n), iy * n + ix)

        key = expert_ids.reshape(n_copy) * n_copy + jnp.arange(n_copy, dtype=jnp.int32)
        skey, sgate = lax.sort((key, gate_prob.reshape(n_copy)), num_keys=1, is_stable=False)
        stok = (lax.rem(skey, n_copy) // top_k).astype(F32)
        tab = jnp.stack([stok, sgate])
        lo = dst_chip * exp_chip
        hot_shift = hot_rows * exp_chip // base_rows
        by_block = tab.reshape(2, n_copy // base_rows, base_rows)
        e_id = jnp.arange(n_exp)[None, :, None]
        base = jnp.where(e_id < lo, by_block[:, :n_exp], by_block[:, hot_shift:hot_shift + n_exp])
        hot = lax.dynamic_slice(tab, (0, lo * base_rows), (2, exp_chip * (base_rows + hot_rows)))
        hot = hot.reshape(2, exp_chip, base_rows + hot_rows)
        base = lax.dynamic_update_slice(base, hot[:, :, :base_rows], (0, lo, 0))
        base = base.reshape(2, n, n, n_core, exp_dev, base_rows)
        base = lax.dynamic_slice_in_dim(jnp.concatenate([base, base], axis=1), iy, n, axis=1)
        base = lax.dynamic_slice_in_dim(jnp.concatenate([base, base], axis=2), ix, n, axis=2)
        base = jnp.where(core == 0, base, base[:, :, :, ::-1])
        hot = hot[:, :, base_rows:].reshape(2, n_core, exp_dev, hot_rows)
        hot = jnp.where(core == 0, hot, hot[:, ::-1])
        n_row = n * n_core * base_rows
        tx = jnp.stack([base.transpose(2, 4, 0, 1, 3, 5).reshape(n, exp_dev * 2, n_row), base.transpose(1, 4, 0, 2, 3, 5).reshape(n, exp_dev * 2, n_row)])
        tx = jnp.pad(tx, ((0, 0), (0, 0), (0, 8 - exp_dev * 2), (0, 0)))
        ht = hot.reshape(2 * exp_chip, hot_rows)

        p0, v = layer(n, n_core, base_rows, hot_rows, tokens, tx, ht, w_gate, w_up, w_down)
        return last_sum(p0, v)

    return jax.shard_map(device_body, mesh=mesh, in_specs=(TOKEN_SPEC, TOKEN_SPEC, TOKEN_SPEC, EXPERT_SPEC, EXPERT_SPEC, EXPERT_SPEC), out_specs=TOKEN_SPEC, check_vma=False)
```

profile of v0, /device:TPU:97, one launch (start us, length us, event | category | flops | bytes accessed | tf_op | source)
XLA Modules:
  0.0 400.1 jit_solution(15453526051285002366)
XLA Ops:
  0.0 0.7 broadcast_multiply_fusion
  0.7 0.2 copy.8
  0.9 0.2 mul.22
  1.1 0.9 copy.9
  2.0 0.2 reshape.28
  2.2 5.7 %sort.15 = (s32[6144]{0:T(1024)S(1)}, f32[6144]{0:T(1024)S(1)}) sort(s32[6144]{0:T(1024)S(1)} %iota_add_fusion, f32[6144]{0:T(1024)S(1)} %reshape.28), dimensions={0}, to_apply=%region_0.1 | sort | flops 79872 | bytes 98304 | tf_op jit(solution)/shard_map/sort | solution.py:594
  7.9 0.1 fusion.7
  8.1 0.1 reshape.29
  8.1 0.1 slice.19
  8.3 0.6 reshape.32.ht_ref
  8.9 0.1 stack.18
  9.0 0.1 stack.19
  9.0 0.1 slice_select_fusion
  9.1 0.1 fusion.1
  9.2 0.1 fusion
  9.4 0.1 stack_reshape.6
  9.5 0.1 stack_reshape.7
  9.7 0.7 select_maximum_fusion.tx_ref
  10.3 382.8 %layer.1 = (bf16[2,768,1024]{2,1,0:T(8,128)(2,1)}, bf16[2,2,768,1024]{3,2,1,0:T(8,128)(2,1)}, bf16[2,2048,1024]{2,1,0:T(8,128)(2,1)}, bf16[2,2,2048,1024]{3,2,1,...) custom-call(bf16[768,2048]{1,0:T(8,128)(2,1)} %tok_ref.1, ...), custom_call_target="tpu_custom_call" | custom-call | tf_op jit(solution)/shard_map/layer/pallas_call | solution.py:531
  393.2 6.9 %last_sum.1 = bf16[768,2048]{1,0:T(8,128)(2,1)} custom-call(bf16[2,768,1024]{2,1,0:T(8,128)(2,1)} %get-tuple-element.11.p_ref, bf16[2,2,768,1024]{3,2,1,0:T(8,128)(2,1)} %get-tuple-element.12.v_ref), custom_call_target="tpu_custom_call" | custom-call | tf_op jit(solution)/shard_map/last_sum/pallas_call | solution.py:562
  (11 shorter events, 0.2 us)
where the time goes:
time: 401 us; the launch traced here: 400 us
  Pallas kernels  390 us (97%)
  other arithmetic  7.5 us (2%)
    pallas_call x1, Pallas kernels, layer(): pl.pallas_call(functools.partial(layer_kernel, n, n_core, exp_dev, base_r...  383 us

commit v1 on v0

--- a/solution.py
+++ b/solution.py
@@ -144,7 +144,7 @@
 
     @pl.loop(0, n * n_core)
     def _(t):
-        dc, dy = t // n, lax.rem(t, n)
+        dc, dy = t // n, lax.rem(t + 1, n)
         j = dy * n_core + dc
         rows1 = rows_at(start + j * piece, piece)
         rows2 = [None] * n
@@ -164,24 +164,29 @@
         def _():
             return_keep(0, x_ref, start, dst_ref, s_sem, piece).start()
 
-        @pl.when(dy == n - 1)
+        def part(dx):
+            jx = dx * n_core + dc
+            first_row = place(dy, n) * base_rows
+            dev = here.dev(**{AXES[1][1]: n - dx, 'core': dc})
+            src = x_ref.at[1, rows_at(start + jx * piece + first_row, base_rows)]
+            return remote(src, dst_ref.at[1, rows_at(jx * piece + first_row, base_rows)], s_sem.at[1, jx], r_sem.at[1, jx], dev)
+
+        for dx in range(n - 1, 0, -1):
+            part(dx).start()
+
+        @pl.when(dc > 0)
         def _():
-            for dx in range(n - 1, 0, -1):
-                return_copy(here, 1, dx * n_core + dc, x_ref, start, dst_ref, s_sem, r_sem, piece).start()
-
-            @pl.when(dc > 0)
-            def _():
-                return_copy(here, 1, dc, x_ref, start, dst_ref, s_sem, r_sem, piece).start()
-
-            @pl.when(dc == 0)
-            def _():
-                return_keep(1, x_ref, start, dst_ref, s_sem, piece).start()
+            part(0).start()
+
+        @pl.when((dc == 0) & (dy == 0))
+        def _():
+            return_keep(1, x_ref, start, dst_ref, s_sem, piece).start()
 
 
 def layer_kernel(n, n_core, exp_dev, base_rows, hot_rows, tok_ref, tx_ref, ht_ref, wg_ref, wu_ref, wd_ref,
-                 p0_ref, v_ref, re_ref, q_ref, hs_ref, u_ref, hy_ref,
+                 p0_ref, v_ref, re_ref, q_ref, hs_ref, hy_ref,
                  rx_ref, htr_ref, g_ref, hb_ref, m_ref, w_ref,
-                 own_sem, w_sem, tab_s, tab_r, g_s, g_r, d_s, d_r, hot_s, hot_r, swap_s, swap_r, x_sem, ret_s, ret_r, sum_s, sum_r, ring_s, ring_r, load_sem):
+                 own_sem, w_sem, tab_s, tab_r, g_s, g_r, d_s, d_r, hot_s, hot_r, swap_s, swap_r, x_sem, ret_s, ret_r, sum_s, sum_r, ring_s, ring_r, load_sem, free_sem):
     here = Here(n, n_core)
     tok_dev, d_model = tok_ref.shape
     d_ff = wg_ref.shape[2]
@@ -395,6 +400,10 @@
         for c in sums:
             c.start()
 
+    for h in range(2):
+        for i, by in enumerate((-1, 1)):
+            pl.semaphore_signal(free_sem.at[h, i], inc=1, device_id=here.dev(**{AXES[h][0]: by}), device_id_type=MESH)
+
     for c in first + far:
         c.wait_send()
 
@@ -422,8 +431,13 @@
     def p_rows(h, s):
         return rows_at((h * n + s) * tok_dev, tok_dev)
 
-    def p_half(h, s, part):
-        return pl.ds((h * n + s) * tok_dev + part * half, half)
+    quarter = half // 2
+
+    def quarters(part):
+        return [pl.ds((2 * part + q) * quarter, quarter) for q in range(2)]
+
+    def p_part(h, s, part):
+        return pl.ds((h * n + s) * tok_dev + part.start, part.size)
 
     def spread(h, s):
         acc = None
@@ -436,22 +450,26 @@
     ring = []
 
     def send(h, i, s, part, dst, by, start=True):
-        c = remote(w_ref.at[p_half(h, s, part)], dst, ring_s.at[h, i], ring_r.at[h, i], here.dev(**{AXES[h][0]: by}))
+        c = remote(w_ref.at[p_part(h, s, part)], dst, ring_s.at[h, i], ring_r.at[h, i], here.dev(**{AXES[h][0]: by}))
         if start:
             c.start()
         ring.append(c)
         return c
 
-    tops = []
+    tops = [[], []]
     for h in range(2):
         w_ref[p_rows(h, far_slot)] = spread(h, far_slot).astype(BF16)
-        tops.append(send(h, 0, far_slot, 0, u_ref.at[h, lo], 1, False))
-        tops.append(send(h, 1, far_slot, 1, u_ref.at[h, hi], -1, False))
+        for q in range(2):
+            tops[h].append(send(h, q, far_slot, quarters(0)[q], m_ref.at[h, quarters(0)[q]], 1, False))
+            tops[h].append(send(h, 2 + q, far_slot, quarters(1)[q], m_ref.at[h, quarters(1)[q]], -1, False))
+
+        for i in range(2):
+            pl.semaphore_wait(free_sem.at[h, i], 1)
 
         @pl.when(jnp.logical_not(middle))
         def _():
-            tops[2 * h].start()
-            tops[2 * h + 1].start()
+            for c in tops[h]:
+                c.start()
 
     last = []
     for s, part, by in ((n - 1, 1, 1), (1, 0, -1)):
@@ -460,26 +478,26 @@
             w_ref[p_rows(h, s)] = spread(h, s).astype(BF16)
 
         for h in range(2):
-            last.append(send(h, 2 + part, s, part, v_ref.at[h, 1 - part, (lo, hi)[part]], by))
-
-    def load(ref, h, rows, start):
-        c = pltpu.make_async_copy(ref.at[h, rows], m_ref.at[h, pl.ds(start, half)], own_sem.at[h])
-        c.start()
-        c.wait()
-        return m_ref[h, pl.ds(start, half)].astype(F32)
-
-    def add_to(h, s, part, more):
-        rows = p_half(h, s, part)
-        w_ref[rows] = (w_ref[rows].astype(F32) + more).astype(BF16)
+            last.append(send(h, 4 + part, s, (lo, hi)[part], v_ref.at[h, 1 - part, (lo, hi)[part]], by))
+
+    def add_to(h, s, part, start=0):
+        rows = p_part(h, s, part)
+        more = m_ref[h, pl.ds(start + part.start, part.size)]
+        w_ref[rows] = (w_ref[rows].astype(F32) + more.astype(F32)).astype(BF16)
 
     @pl.when(middle)
     def _():
+        loads = [pltpu.make_async_copy(hs_ref.at[h], m_ref.at[h, pl.ds(hot_dev, tok_dev)], own_sem.at[h]) for h in range(2)]
         for h in range(2):
             sums[h].wait_recv()
-            add_to(h, far_slot, 0, load(hs_ref, h, lo, 0))
-            tops[2 * h].start()
-            add_to(h, far_slot, 1, load(hs_ref, h, hi, 0))
-            tops[2 * h + 1].start()
+            loads[h].start()
+        for h in range(2):
+            loads[h].wait()
+            for q in range(2):
+                add_to(h, far_slot, quarters(0)[q], hot_dev)
+                tops[h][2 * q].start()
+                add_to(h, far_slot, quarters(1)[q], hot_dev)
+                tops[h][2 * q + 1].start()
 
     own_hot = jnp.where(moved, 0.0, 1.0).astype(F32)
 
@@ -487,19 +505,20 @@
     def _(h):
         w_ref[p_rows(h, 0)] = (spread(h, 0) + own_hot * hb_ref[h].astype(F32)).astype(BF16)
 
-    out = [pltpu.make_async_copy(w_ref.at[p_rows(h, 0)], p0_ref.at[h], x_sem) for h in range(2)]
-    out[0].start()
-    out[0].wait()
-    out[1].start()
-    for h in range(2):
-        tops[2 * h].wait_recv()
-        add_to(h, n - 1, 0, load(u_ref, h, lo, 0))
-        last.append(send(h, 4, n - 1, 0, v_ref.at[h, 0, lo], 1))
-        tops[2 * h + 1].wait_recv()
-        add_to(h, 1, 1, load(u_ref, h, hi, 0))
-        last.append(send(h, 5, 1, 1, v_ref.at[h, 1, hi], -1))
-
-    out[1].wait()
+    out = [pltpu.make_async_copy(w_ref.at[p_rows(h, 0)], p0_ref.at[h], own_sem.at[h]) for h in range(2)]
+    for c in out:
+        c.start()
+    for q in range(2):
+        for h in range(2):
+            tops[h][2 * q].wait_recv()
+            add_to(h, n - 1, quarters(0)[q])
+            last.append(send(h, 6 + q, n - 1, quarters(0)[q], v_ref.at[h, 0, quarters(0)[q]], 1))
+            tops[h][2 * q + 1].wait_recv()
+            add_to(h, 1, quarters(1)[q])
+            last.append(send(h, 8 + q, 1, quarters(1)[q], v_ref.at[h, 1, quarters(1)[q]], -1))
+
+    for c in out:
+        c.wait()
     for c in tabs + back:
         c.wait_send()
     for h in range(2):
@@ -530,9 +549,9 @@
     hbm = lambda *shape: jax.ShapeDtypeStruct(shape, BF16)
     return pl.pallas_call(
         functools.partial(layer_kernel, n, n_core, exp_dev, base_rows, hot_rows),
-        out_shape=(hbm(2, tok_dev, dh), hbm(2, 2, tok_dev, dh), hbm(2, n_row, dh), hbm(exp_dev, 2, n_row, dh), hbm(2, tok_dev, dh), hbm(2, tok_dev, dh), hbm(2, exp_dev * hot_rows, dh)),
+        out_shape=(hbm(2, tok_dev, dh), hbm(2, 2, tok_dev, dh), hbm(2, n_row, dh), hbm(exp_dev, 2, n_row, dh), hbm(2, tok_dev, dh), hbm(2, exp_dev * hot_rows, dh)),
         in_specs=[any_, vm, vm, any_, any_, any_],
-        out_specs=(any_,) * 7,
+        out_specs=(any_,) * 6,
         scratch_shapes=[
             pltpu.VMEM(tx.shape, F32),
             pltpu.VMEM(ht.shape, F32),
@@ -542,7 +561,7 @@
             pltpu.VMEM((max(2 * d_model + 2 * d_ff, 2 * n * tok_dev), dh), BF16),
             dma((2,)), dma((4,)), dma((2 * n,)), dma((2 * n,)), dma((2, 6)), dma((2, 6)),
             dma((2, exp_dev, n_dst, 2)), dma((2, exp_dev, n_dst, 2)), dma((2,)), dma((2,)), dma((4,)), dma((4,)), dma,
-            dma((exp_dev, 2, n_dst)), dma((exp_dev, 2, n_dst)), dma((2,)), dma((2,)), dma((2, 6)), dma((2, 6)), dma((2, n_dst)),
+            dma((exp_dev, 2, n_dst)), dma((exp_dev, 2, n_dst)), dma((2,)), dma((2,)), dma((2, 10)), dma((2, 10)), dma((2, n_dst)), pltpu.SemaphoreType.REGULAR((2, 2)),
         ],
         compiler_params=pltpu.CompilerParams(vmem_limit_bytes=VMEM_LIMIT, collective_id=0, has_side_effects=True),
         name='layer',

time: 401 us -> 393 us (0.980)
  Pallas kernels: 390 us -> 383 us
    pallas_call x1, Pallas kernels: 383 us -> 376 us  [layer(): pl.pallas_call(functools.partial(layer_kernel, n, n_core, exp_dev, base_r...]
where the time goes in v1:
time: 393 us
  Pallas kernels  383 us (97%)
  other arithmetic  7.5 us (2%)
    pallas_call x1, Pallas kernels, layer(): pl.pallas_call(functools.partial(layer_kernel, n, n_core, exp_dev, base_r...  376 us

profile of v1, /device:TPU:97, one launch (start us, length us, event | category | flops | bytes accessed | tf_op | source)
XLA Modules:
  0.0 392.9 jit_solution(6555750153691886484)
XLA Ops:
  0.0 0.7 broadcast_multiply_fusion
  0.7 0.2 copy.8
  0.9 0.2 mul.22
  1.1 0.9 copy.9
  2.0 0.2 reshape.28
  2.2 5.7 %sort.15 = (s32[6144]{0:T(1024)S(1)}, f32[6144]{0:T(1024)S(1)}) sort(s32[6144]{0:T(1024)S(1)} %iota_add_fusion, f32[6144]{0:T(1024)S(1)} %reshape.28), dimensions={0}, to_apply=%region_0.1 | sort | flops 79872 | bytes 98304 | tf_op jit(solution)/shard_map/sort | solution.py:613
  7.9 0.1 fusion.7
  8.1 0.1 reshape.29
  8.1 0.1 slice.19
  8.3 0.6 reshape.32.ht_ref
  8.9 0.1 stack.18
  9.0 0.1 stack.19
  9.0 0.1 slice_select_fusion
  9.1 0.1 fusion.1
  9.2 0.1 fusion
  9.4 0.1 stack_reshape.6
  9.5 0.1 stack_reshape.7
  9.7 0.7 select_maximum_fusion.tx_ref
  10.3 375.6 %layer.1 = (bf16[2,768,1024]{2,1,0:T(8,128)(2,1)}, bf16[2,2,768,1024]{3,2,1,0:T(8,128)(2,1)}, bf16[2,2048,1024]{2,1,0:T(8,128)(2,1)}, bf16[2,2,2048,1024]{3,2,1,...) custom-call(bf16[768,2048]{1,0:T(8,128)(2,1)} %tok_ref.1, ...), custom_call_target="tpu_custom_call" | custom-call | tf_op jit(solution)/shard_map/layer/pallas_call | solution.py:550
  386.0 6.9 %last_sum.1 = bf16[768,2048]{1,0:T(8,128)(2,1)} custom-call(bf16[2,768,1024]{2,1,0:T(8,128)(2,1)} %get-tuple-element.11.p_ref, bf16[2,2,768,1024]{3,2,1,0:T(8,128)(2,1)} %get-tuple-element.12.v_ref), custom_call_target="tpu_custom_call" | custom-call | tf_op jit(solution)/shard_map/last_sum/pallas_call | solution.py:581
  (11 shorter events, 0.2 us)

commit v2 on v1

--- a/solution.py
+++ b/solution.py
@@ -282,15 +282,15 @@
     pick(far_slot, 0, 2)
     send_rows(0, piece - base_rows, base_rows, 1, True)
 
+    pick(far_slot, 2, 2 * exp_dev)
+    send_rows(1, 0, piece, 0, True)
+
     hot = [remote(g_ref.at[h, slot(far_slot)], hb_ref.at[h], hot_s.at[h], hot_r.at[h], here.dev(**{AXES[h][1]: n // 2})) for h in range(2)]
 
     @pl.when(middle)
     def _():
         for c in hot:
             c.start()
-
-    pick(far_slot, 2, 2 * exp_dev)
-    send_rows(1, 0, piece, 0, True)
 
     def done_send(c):
         if c.is_remote:
@@ -307,6 +307,17 @@
     for c in sends[0]:
         done_recv(c)
     base_ffn(here, m_ref, recv0, q_ref.at[0], w_ref, d_model, d_ff, base_rows, ret_s.at[0], ret_r.at[0])
+
+    weights = load_weights(exp_dev - 1, wg_ref, wu_ref, wd_ref, w_ref, w_sem)
+    for c in sends[1]:
+        done_recv(c)
+        done_send(c)
+    x_in = pltpu.make_async_copy(re_ref, m_ref.at[:, pl.ds(n_row, n_row)], x_sem)
+    x_in.start()
+    x_in.wait()
+    for c in weights:
+        c.wait()
+    base_ffn(here, m_ref, n_row, q_ref.at[1], w_ref, d_model, d_ff, base_rows, ret_s.at[1], ret_r.at[1])
 
     @pl.when(jnp.logical_not(moved))
     def _():
@@ -341,29 +352,25 @@
     tiles = hot_rows // piece
 
     @pl.loop(0, exp_dev)
-    def _(e):
-        @pl.when(e > 0)
+    def _(i):
+        e = exp_dev - 1 - i
+
+        @pl.when(i > 0)
         def _():
             for c in load_weights(e, wg_ref, wu_ref, wd_ref, w_ref, w_sem):
                 c.wait()
 
         @pl.loop(0, n_core * tiles)
         def _(k):
-            rows = rows_at((k // tiles) * land + e * hot_rows + lax.rem(k, tiles) * piece, piece)
+            @pl.when((i == exp_dev - 1) & (k == tiles))
+            def _():
+                for c in back:
+                    c.start()
+
+            rows = rows_at((1 - k // tiles) * land + e * hot_rows + lax.rem(k, tiles) * piece, piece)
             y1, y2 = gated_mlp(m_ref[0, rows], m_ref[1, rows], w_ref, d_model, d_ff)
             m_ref[0, rows] = y1
             m_ref[1, rows] = y2
-
-    for c in back:
-        c.start()
-
-    for c in sends[1]:
-        done_recv(c)
-        done_send(c)
-    x_in = pltpu.make_async_copy(re_ref, m_ref.at[:, pl.ds(n_row, n_row)], x_sem)
-    x_in.start()
-    x_in.wait()
-    base_ffn(here, m_ref, n_row, q_ref.at[1], w_ref, d_model, d_ff, base_rows, ret_s.at[1], ret_r.at[1])
 
     for h in range(2):
         return_keep(h, m_ref, recv0, q_ref.at[0], ret_s.at[0], piece).wait()

time: 393 us -> 388 us (0.987)
  Pallas kernels: 383 us -> 377 us
    pallas_call x1, Pallas kernels: 376 us -> 370 us  [layer(): pl.pallas_call(functools.partial(layer_kernel, n, n_core, exp_dev, base_r...]
where the time goes in v2:
time: 388 us
  Pallas kernels  377 us (97%)
  other arithmetic  7.5 us (2%)
    pallas_call x1, Pallas kernels, layer(): pl.pallas_call(functools.partial(layer_kernel, n, n_core, exp_dev, base_r...  370 us

profile of v2, /device:TPU:97, one launch (start us, length us, event | category | flops | bytes accessed | tf_op | source)
XLA Modules:
  0.0 387.7 jit_solution(3577628499372619452)
XLA Ops:
  0.0 0.7 broadcast_multiply_fusion
  0.7 0.2 copy.8
  0.9 0.2 mul.22
  1.1 0.9 copy.9
  2.0 0.2 reshape.28
  2.2 5.7 %sort.15 = (s32[6144]{0:T(1024)S(1)}, f32[6144]{0:T(1024)S(1)}) sort(s32[6144]{0:T(1024)S(1)} %iota_add_fusion, f32[6144]{0:T(1024)S(1)} %reshape.28), dimensions={0}, to_apply=%region_0.1 | sort | flops 79872 | bytes 98304 | tf_op jit(solution)/shard_map/sort | solution.py:620
  7.9 0.1 fusion.7
  8.1 0.1 reshape.29
  8.1 0.1 slice.19
  8.3 0.6 reshape.32.ht_ref
  8.9 0.1 stack.18
  9.0 0.1 stack.19
  9.0 0.1 slice_select_fusion
  9.1 0.1 fusion.1
  9.2 0.1 fusion
  9.4 0.1 stack_reshape.6
  9.5 0.1 stack_reshape.7
  9.7 0.7 select_maximum_fusion.tx_ref
  10.3 370.4 %layer.1 = (bf16[2,768,1024]{2,1,0:T(8,128)(2,1)}, bf16[2,2,768,1024]{3,2,1,0:T(8,128)(2,1)}, bf16[2,2048,1024]{2,1,0:T(8,128)(2,1)}, bf16[2,2,2048,1024]{3,2,1,...) custom-call(bf16[768,2048]{1,0:T(8,128)(2,1)} %tok_ref.1, ...), custom_call_target="tpu_custom_call" | custom-call | tf_op jit(solution)/shard_map/layer/pallas_call | solution.py:557
  380.8 6.9 %last_sum.1 = bf16[768,2048]{1,0:T(8,128)(2,1)} custom-call(bf16[2,768,1024]{2,1,0:T(8,128)(2,1)} %get-tuple-element.11.p_ref, bf16[2,2,768,1024]{3,2,1,0:T(8,128)(2,1)} %get-tuple-element.12.v_ref), custom_call_target="tpu_custom_call" | custom-call | tf_op jit(solution)/shard_map/last_sum/pallas_call | solution.py:588
  (11 shorter events, 0.2 us)
